TPU v7x, 128 devices: a whole 4x4x4 slice. The times are simulated.
128 devices in a mesh: dp: 32 (over z, y, core), tensor: 4 (over x).
Axes of the slice: x: 4, y: 4, z: 4, core: 2. Of those that a mesh axis runs over, the one named last changes fastest.
Arguments:
- tokens: bfloat16 [12288, 2880], P('dp', 'tensor'), may hold values from -6 to 6
- out_grad: bfloat16 [12288, 2880], P('dp', 'tensor'), may hold values from -6 to 6
- route_probs: bfloat16 [12288, 4], P('dp'), may hold values from 0.099609375 to 1
- expert_ids: int32 [12288, 4], P('dp'), may hold values from 0 to 127, all different within a row; in each aligned block of 384 rows (0 to 383, 384 to 767, ...) at most 18 rows name the same one
- placement_map: int32 [128], replicated, may hold values from 0 to 127, each once
- w_gate: bfloat16 [32, 2880, 2880], P('dp', None, 'tensor'), may hold values from -0.109375 to 0.109375
- w_up: bfloat16 [32, 2880, 2880], P('dp', None, 'tensor'), may hold values from -0.109375 to 0.109375
- w_down: bfloat16 [32, 2880, 2880], P('dp', 'tensor'), may hold values from -0.109375 to 0.109375
Outputs:
- input_grad: bfloat16 [12288, 2880], P('dp', 'tensor')
- gate_grad: bfloat16 [32, 2880, 2880], P('dp', None, 'tensor')
- up_grad: bfloat16 [32, 2880, 2880], P('dp', None, 'tensor')
- down_grad: bfloat16 [32, 2880, 2880], P('dp', 'tensor')
- prob_grad: bfloat16 [12288, 4], P('dp')
Inputs may be any that keep to these rules, and one draw needn't show every extreme that they name: `expert_ids`: each row names 4 different experts. In the rows of one index of dp no expert is named by more than 18 rows, a bound that some block reaches. `placement_map`: A permutation: every value is taken by exactly one expert.
All inputs are finite; a program needn't handle non-finite values.
Results may differ from a plain program's by a relative error of at most 0.011.
Values may be sent and summed in bfloat16 or wider, within the bound.
A program may use at most 128 MiB of HBM per device.

v0:
```python
import functools

import jax
import jax.numpy as jnp
import numpy as np
from jax import lax
from jax.experimental import pallas as pl
from jax.experimental.pallas import tpu as pltpu
from jax.sharding import PartitionSpec as P

SLOPE = 1.702
MESH = pl.DeviceIdType.MESH
NDP, NT = 32, 4
CAP = 18
TOK, F, FP = 384, 720, 768
SB, DOFF = 40, 20
RB = 24
PL = 8
G = 4
GR = PL * CAP
SRC_ORDER = (0, 1, 3, 2)
DST_ORDER = (0, 3, 1, 2)
LANES = (((1,), (1,)), ((), ()))
F32, BF16 = jnp.float32, jnp.bfloat16


def dot(a, b):
    return jnp.dot(a, b, preferred_element_type=F32)


def dot_lanes(a, b):
    return lax.dot_general(a, b, LANES, preferred_element_type=F32)


def iota(shape, dim):
    return lax.broadcasted_iota(jnp.int32, shape, dim)


def owner_table(pcol):
    return jnp.where(pcol == 4 * iota((128, 128), 1), 1.0, 0.0).astype(BF16)


def route_ranks(ids, table):
    hit = jnp.zeros((TOK, 128), F32)
    for k in range(4):
        hit += jnp.where(ids[:, k : k + 1] == iota((TOK, 128), 1), 1.0, 0.0)
    member = dot(hit.astype(BF16), table)
    lower = jnp.where(iota((TOK, TOK), 0) > iota((TOK, TOK), 1), 1.0, 0.0).astype(BF16)
    rank = dot(lower, member.astype(BF16))
    return jnp.where(member > 0.5, rank, -1.0).astype(BF16)


def comm_kernel(
    ids_ref, pcol_ref, probs_ref, tok_ref, og_ref, c40_ref, cx_ref, cd_ref, rx_ref, wg_hbm, wu_hbm, wd_hbm,
    x_out, d_out, dg_out, du_out, pa_out, back_out,
    send, recv, xb, db, wg, wu, wd, wdq, acc_g, acc_u, acc_d, dg, du, pa, prob, dxs, far_in, left_in, right_in, ret, ret_in,
    w_sem, a2a_s, a2a_r, gat_s, gat_r, far_s, far_r, out_s, left_r, right_r, ret_s, ret_r, o_sem,
):
    me = lax.axis_index("dp")
    t = lax.axis_index("tensor")
    z = me // PL
    right, left, far = (t + 1) % NT, (t + 3) % NT, (t + 2) % NT

    barrier = pltpu.get_barrier_semaphore()

    def greet(d, c):
        @pl.when(d != me)
        def _():
            pl.semaphore_signal(barrier, inc=1, device_id=(d, t), device_id_type=MESH)

        return c

    lax.fori_loop(0, NDP, greet, 0)
    for nb in (left, right):
        pl.semaphore_signal(barrier, inc=1, device_id=(me, nb), device_id_type=MESH)

    weights = [
        pltpu.make_async_copy(src, dst, w_sem.at[i])
        for i, (src, dst) in enumerate(((wg_hbm, wg), (wu_hbm, wu), (wd_hbm, wd)))
    ]
    for w in weights:
        w.start()

    ids = ids_ref[...]
    table = owner_table(pcol_ref[...])
    probs = probs_ref[...].astype(F32)
    ranks = route_ranks(ids, table)
    pw = jnp.zeros((TOK, 128), F32)
    for k in range(4):
        pw += jnp.where(ids[:, k : k + 1] == iota((TOK, 128), 1), probs[:, k : k + 1], 0.0)
    owner_p = dot(pw.astype(BF16), table).astype(BF16)

    def plane(order, i):
        return (z + order[i]) % G

    def build(zd):
        block, jx, jd = c40_ref[:, 0:1], c40_ref[:, 1:2], c40_ref[:, 2:3]
        mine = iota((PL * SB, 128), 1) == block + zd * PL
        slots = dot_lanes(jnp.where(mine, 1.0, 0.0).astype(BF16), ranks)
        hot_x = jnp.where(slots == jx.astype(F32), 1.0, 0.0).astype(BF16)
        hot_d = jnp.where(slots == jd.astype(F32), 1.0, 0.0).astype(BF16)
        rows = dot(hot_x, tok_ref[...]) + dot(hot_d, og_ref[...])
        p = jnp.sum(jnp.where(mine, dot(hot_x, owner_p), 0.0), axis=1, keepdims=True)
        for j in range(PL):
            part = slice(j * SB, (j + 1) * SB)
            send[zd * PL + j, :, 0:F] = rows[part].astype(BF16)
            send[zd * PL + j, :, F:FP] = jnp.broadcast_to(p[part], (SB, FP - F)).astype(BF16)

    def a2a(o):
        return pltpu.make_async_remote_copy(
            src_ref=send.at[o], dst_ref=recv.at[me], send_sem=a2a_s.at[o], recv_sem=a2a_r.at[me],
            device_id=(o, t), device_id_type=MESH)

    def a2a_in(s):
        return pltpu.make_async_remote_copy(
            src_ref=send.at[s], dst_ref=recv.at[s], send_sem=a2a_s.at[s], recv_sem=a2a_r.at[s],
            device_id=(s, t), device_id_type=MESH)

    def others(first, act):
        def body(j, c):
            o = first + j

            @pl.when(o != me)
            def _():
                act(o)

            return c

        lax.fori_loop(0, PL, body, 0)

    for i in range(G):
        zd = plane(DST_ORDER, i)
        build(zd)
        if i == 0:
            pl.semaphore_wait(barrier, NDP - 1 + 2)
            recv[me] = send[me]
        others(zd * PL, lambda o: a2a(o).start())

    for w in weights:
        w.wait()

    def quarter_rows(r, c):
        rows = pl.ds(pl.multiple_of(r * 144, 16), 144)
        for q in range(NT):
            wdq[q, rows, 0:F] = wd[rows, q * F : (q + 1) * F]
        return c

    lax.fori_loop(0, F // 144, quarter_rows, 0)

    def gat(kind, i, ref, q, to):
        zs = plane(SRC_ORDER, i)
        return pltpu.make_async_remote_copy(
            src_ref=ref.at[q, zs], dst_ref=ref.at[q, zs], send_sem=gat_s.at[kind, i], recv_sem=gat_r.at[kind, i],
            device_id=(me, to), device_id_type=MESH)

    def gat_out(kind, i):
        return (
            lambda: gat(0, i, xb, t, right), lambda: gat(1, i, xb, t, left),
            lambda: gat(2, i, db, t, right), lambda: gat(3, i, db, t, left),
            lambda: gat(4, i, xb, left, right), lambda: gat(5, i, db, right, left),
        )[kind]()

    def gat_in(kind, i):
        return (
            lambda: gat(0, i, xb, left, right), lambda: gat(1, i, xb, right, left),
            lambda: gat(2, i, db, left, right), lambda: gat(3, i, db, right, left),
            lambda: gat(4, i, xb, far, right), lambda: gat(5, i, db, far, left),
        )[kind]()

    def stage_d(i):
        zs = plane(SRC_ORDER, i)
        others(zs * PL, lambda s: a2a_in(s).wait_recv())
        got = recv[pl.ds(zs * PL, PL)].reshape(PL * SB, FP)
        xb[t, zs] = dot(cx_ref[...], got).astype(BF16)
        db[t, zs] = dot(cd_ref[...], got).astype(BF16)
        for kind in range(4):
            gat_out(kind, i).start()

    def stage_f(i):
        gat_in(0, i).wait_recv()
        gat_out(4, i).start()
        gat_in(3, i).wait_recv()
        gat_out(5, i).start()

    def rs_far(i):
        zs = plane(SRC_ORDER, i)
        return pltpu.make_async_remote_copy(
            src_ref=dxs.at[0, zs], dst_ref=far_in.at[zs], send_sem=far_s.at[i], recv_sem=far_r.at[i],
            device_id=(me, left if i % 2 == 0 else right), device_id_type=MESH)

    def rs_left(i):
        zs = plane(SRC_ORDER, i)
        return pltpu.make_async_remote_copy(
            src_ref=dxs.at[1, zs], dst_ref=right_in.at[zs], send_sem=out_s.at[0, i], recv_sem=right_r.at[i],
            device_id=(me, left), device_id_type=MESH)

    def rs_right(i):
        zs = plane(SRC_ORDER, i)
        return pltpu.make_async_remote_copy(
            src_ref=dxs.at[3, zs], dst_ref=left_in.at[zs], send_sem=out_s.at[1, i], recv_sem=left_r.at[i],
            device_id=(me, right), device_id_type=MESH)

    def stage_c(i):
        zs = plane(SRC_ORDER, i)
        for kind in (1, 2, 4, 5):
            gat_in(kind, i).wait_recv()
        acc_g[...] = jnp.zeros_like(acc_g)
        acc_u[...] = jnp.zeros_like(acc_u)
        acc_d[...] = jnp.zeros_like(acc_d)

        def forward(q, c):
            feats = pl.ds(pl.multiple_of(q * F, 16), F)
            xq = xb[q, zs, :, 0:F]
            acc_g[...] += dot(xq, wg[feats, :])
            acc_u[...] += dot(xq, wu[feats, :])
            acc_d[...] += dot_lanes(db[q, zs, :, 0:F], wdq[q, :, 0:F])
            return c

        lax.fori_loop(0, NT, forward, 0)

        def elementwise(r, c):
            rows = pl.ds(pl.multiple_of(r * 16, 16), 16)
            gate, up, back = acc_g[rows, :], acc_u[rows, :] + 1.0, acc_d[rows, :]
            p = xb[t, zs, rows, F : F + 1].astype(F32)
            sig = 1.0 / (1.0 + jnp.exp(-SLOPE * gate))
            swish = gate * sig
            active = (swish * up).astype(BF16).astype(F32)
            prob[rows, :] = jnp.broadcast_to(jnp.sum(active * back, axis=1, keepdims=True), (16, 128))
            delta = p * back
            pa[zs, rows, 0:F] = (p * active).astype(BF16)
            dg[zs, rows, 0:F] = (delta * up * (sig + SLOPE * swish * (1.0 - sig))).astype(BF16)
            du[zs, rows, 0:F] = (delta * swish).astype(BF16)
            return c

        lax.fori_loop(0, GR // 16, elementwise, 0)

        def backward(r, c):
            q = (t + 2 + r) % NT
            feats = pl.ds(pl.multiple_of(q * F, 16), F)
            part = dot_lanes(dg[zs, :, 0:F], wg[feats, :]) + dot_lanes(du[zs, :, 0:F], wu[feats, :])
            dxs[r, zs, :, 0:F] = part.astype(BF16)
            dxs[r, zs, :, F:FP] = prob[:, 0 : FP - F].astype(BF16)
            return c

        lax.fori_loop(0, NT, backward, 0)
        rs_far(i).start()
        if i % 2 == 0:
            rs_right(i).start()
        else:
            rs_left(i).start()

    def stage_s(i):
        zs = plane(SRC_ORDER, i)
        rs_far(i).wait()
        role = 1 if i % 2 == 0 else 3
        dxs[role, zs] = (dxs[role, zs].astype(F32) + far_in[zs].astype(F32)).astype(BF16)
        if i % 2 == 0:
            rs_left(i).start()
        else:
            rs_right(i).start()

    def back(s):
        return pltpu.make_async_remote_copy(
            src_ref=ret.at[s], dst_ref=ret_in.at[me], send_sem=ret_s.at[s], recv_sem=ret_r.at[me],
            device_id=(s, t), device_id_type=MESH)

    def back_in(o):
        return pltpu.make_async_remote_copy(
            src_ref=ret.at[o], dst_ref=ret_in.at[o], send_sem=ret_s.at[o], recv_sem=ret_r.at[o],
            device_id=(o, t), device_id_type=MESH)

    def stage_e(i):
        zs = plane(SRC_ORDER, i)
        rs_left(i).wait()
        rs_right(i).wait()
        total = dxs[2, zs].astype(F32) + left_in[zs].astype(F32) + right_in[zs].astype(F32)
        rows = dot(rx_ref[...], total.astype(BF16))
        for j in range(PL):
            ret[zs * PL + j] = rows[j * RB : (j + 1) * RB].astype(BF16)
        if i == 0:
            ret_in[me] = ret[me]
        others(zs * PL, lambda s: back(s).start())

    stage_d(0)
    stage_d(1)
    stage_f(0)
    stage_d(2)
    stage_f(1)
    stage_d(3)
    stage_f(2)
    stage_c(0)
    stage_f(3)
    stage_c(1)
    stage_s(0)
    stage_c(2)
    stage_s(1)
    stage_e(0)
    stage_c(3)
    outs = [
        pltpu.make_async_copy(src, dst, o_sem.at[i])
        for i, (src, dst) in enumerate(((xb, x_out), (db, d_out), (dg, dg_out), (du, du_out), (pa, pa_out)))
    ]
    for o in outs:
        o.start()
    stage_s(2)
    stage_e(1)
    stage_s(3)
    stage_e(2)
    stage_e(3)

    for i in range(G):
        for kind in range(6):
            gat_out(kind, i).wait_send()

    def finish(o, c):
        @pl.when(o != me)
        def _():
            a2a(o).wait_send()
            back(o).wait_send()
            back_in(o).wait_recv()

        return c

    lax.fori_loop(0, NDP, finish, 0)
    for o in outs:
        o.wait()
    last = pltpu.make_async_copy(ret_in, back_out, o_sem.at[5])
    last.start()
    last.wait()


def grads_kernel(
    ids_ref, pcol_ref, c24_ref, x_ref, d_ref, dg_ref, du_ref, pa_ref, back_ref,
    in_grad, gate_grad, up_grad, down_grad, prob_grad,
):
    q = pl.program_id(0)
    xq = x_ref[0, :, 0:F]
    xt = xq.T
    gate_grad[...] = dot(xt, dg_ref[:, 0:F]).astype(BF16)
    up_grad[...] = dot(xt, du_ref[:, 0:F]).astype(BF16)
    pt = pa_ref[:, 0:F].T
    piece = dot(pt, d_ref[0, :, 0:F]).astype(BF16)
    for k in range(NT):

        @pl.when(q == k)
        def _():
            down_grad[:, k * F : (k + 1) * F] = piece

    @pl.when(q == 0)
    def _():
        ids = ids_ref[...]
        table = owner_table(pcol_ref[...])
        ranks = route_ranks(ids, table)
        spread = jnp.where(iota((NDP * RB, 128), 1) == c24_ref[...], 1.0, 0.0).astype(BF16)
        slots = dot_lanes(ranks, spread)
        row = lax.broadcasted_iota(jnp.int32, (TOK, NDP * RB), 1)
        hot = jnp.where(slots == (row % RB).astype(F32), 1.0, 0.0).astype(BF16)
        sums = dot(hot, back_ref[:, 0:F])
        in_grad[...] = sums.astype(BF16)
        ones = dot(hot, jnp.where(iota((NDP * RB, 128), 1) == c24_ref[...], back_ref[:, FP - 128 :][:, 127:128].astype(F32), 0.0).astype(BF16))
        for k in range(4):
            pick = jnp.where(ids[:, k : k + 1] == iota((TOK, 128), 1), 1.0, 0.0).astype(BF16)
            mine = dot(pick, table)
            prob_grad[:, k : k + 1] = jnp.sum(mine * ones, axis=1, keepdims=True).astype(BF16)


def tables():
    r = np.arange(PL * SB)
    jj = r % SB
    jx = np.where(jj < CAP, jj, -5)
    jd = np.where((jj >= DOFF) & (jj < DOFF + CAP), jj - DOFF, -5)
    c40 = np.stack([r // SB, jx, jd], axis=1).astype(np.int32)
    cx = np.zeros((GR, PL * SB), np.float32)
    cd = np.zeros((GR, PL * SB), np.float32)
    rx = np.zeros((PL * RB, GR), np.float32)
    for j in range(PL):
        for k in range(CAP):
            cx[j * CAP + k, j * SB + k] = 1
            cd[j * CAP + k, j * SB + DOFF + k] = 1
            rx[j * RB + k, j * CAP + k] = 1
    c24 = (np.arange(NDP * RB) // RB).astype(np.int32)[:, None]
    return c40, cx, cd, rx, c24


def shards(tokens, out_grad, route_probs, expert_ids, placement_map, w_gate, w_up, w_down):
    c40, cx, cd, rx, c24 = tables()
    pcol = placement_map[:, None]
    vmem = pl.BlockSpec(memory_space=pltpu.VMEM)
    hbm = pl.BlockSpec(memory_space=pl.ANY)
    grp = jax.ShapeDtypeStruct((G, GR, FP), BF16)
    quart = jax.ShapeDtypeStruct((NT, G, GR, FP), BF16)
    dma = pltpu.SemaphoreType.DMA
    x, d, dg, du, pa, back = pl.pallas_call(
        comm_kernel,
        out_shape=(quart, quart, grp, grp, grp, jax.ShapeDtypeStruct((NDP, RB, FP), BF16)),
        in_specs=[vmem] * 9 + [hbm] * 3,
        out_specs=[hbm] * 6,
        scratch_shapes=[
            pltpu.VMEM((NDP, SB, FP), BF16), pltpu.VMEM((NDP, SB, FP), BF16),
            pltpu.VMEM((NT, G, GR, FP), BF16), pltpu.VMEM((NT, G, GR, FP), BF16),
            pltpu.VMEM((NT * F, F), BF16), pltpu.VMEM((NT * F, F), BF16), pltpu.VMEM((F, NT * F), BF16),
            pltpu.VMEM((NT, F, FP), BF16),
            pltpu.VMEM((GR, F), F32), pltpu.VMEM((GR, F), F32), pltpu.VMEM((GR, F), F32),
            pltpu.VMEM((G, GR, FP), BF16), pltpu.VMEM((G, GR, FP), BF16), pltpu.VMEM((G, GR, FP), BF16),
            pltpu.VMEM((GR, 128), F32),
            pltpu.VMEM((NT, G, GR, FP), BF16),
            pltpu.VMEM((G, GR, FP), BF16), pltpu.VMEM((G, GR, FP), BF16), pltpu.VMEM((G, GR, FP), BF16),
            pltpu.VMEM((NDP, RB, FP), BF16), pltpu.VMEM((NDP, RB, FP), BF16),
            dma((3,)), dma((NDP,)), dma((NDP,)), dma((6, G)), dma((6, G)), dma((G,)), dma((G,)),
            dma((2, G)), dma((G,)), dma((G,)), dma((NDP,)), dma((NDP,)), dma((6,)),
        ],
        compiler_params=pltpu.CompilerParams(
            collective_id=0, has_side_effects=True, vmem_limit_bytes=60 * 1024 * 1024
        ),
        name="exchange",
    )(
        expert_ids, pcol, route_probs, tokens, out_grad,
        jnp.asarray(c40), jnp.asarray(cx, BF16), jnp.asarray(cd, BF16), jnp.asarray(rx, BF16),
        w_gate[0], w_up[0], w_down[0],
    )
    rows = G * GR
    whole = lambda *s: pl.BlockSpec(s, lambda q: (0,) * len(s))
    in_grad, gate_grad, up_grad, down_grad, prob_grad = pl.pallas_call(
        grads_kernel,
        grid=(NT,),
        out_shape=(
            jax.ShapeDtypeStruct((TOK, F), BF16),
            jax.ShapeDtypeStruct((NT * F, F), BF16),
            jax.ShapeDtypeStruct((NT * F, F), BF16),
            jax.ShapeDtypeStruct((F, NT * F), BF16),
            jax.ShapeDtypeStruct((TOK, 4), BF16),
        ),
        in_specs=[
            whole(TOK, 4), whole(128, 1), whole(NDP * RB, 1),
            pl.BlockSpec((1, rows, FP), lambda q: (q, 0, 0)), pl.BlockSpec((1, rows, FP), lambda q: (q, 0, 0)),
            whole(rows, FP), whole(rows, FP), whole(rows, FP), whole(NDP * RB, FP),
        ],
        out_specs=[
            whole(TOK, F),
            pl.BlockSpec((F, F), lambda q: (q, 0)),
            pl.BlockSpec((F, F), lambda q: (q, 0)),
            whole(F, NT * F),
            whole(TOK, 4),
        ],
        compiler_params=pltpu.CompilerParams(vmem_limit_bytes=60 * 1024 * 1024),
        name="grads",
    )(
        expert_ids, pcol, jnp.asarray(c24),
        x.reshape(NT, rows, FP), d.reshape(NT, rows, FP),
        dg.reshape(rows, FP), du.reshape(rows, FP), pa.reshape(rows, FP), back.reshape(NDP * RB, FP),
    )
    return (in_grad, gate_grad[None], up_grad[None], down_grad[None], prob_grad)


def solution(mesh):
    in_specs = (
        P("dp", "tensor"), P("dp", "tensor"), P("dp", None), P("dp", None), P(),
        P("dp", None, "tensor"), P("dp", None, "tensor"), P("dp", "tensor", None),
    )
    out_specs = (
        P("dp", "tensor"), P("dp", None, "tensor"), P("dp", None, "tensor"),
        P("dp", "tensor", None), P("dp", None),
    )
    return jax.shard_map(shards, mesh=mesh, in_specs=in_specs, out_specs=out_specs, check_vma=False)
```

profile of v0, /device:TPU:1, one launch (start us, length us, event | category | flops | bytes accessed | tf_op | source)
XLA Modules:
  0.0 182.7 jit_solution(5533850487398599115)
XLA Ops:
  0.6 1.4 copy.26.pcol_ref
  2.0 1.5 copy.22.probs_ref
  3.5 1.5 copy.25.ids_ref
  5.0 2.1 %copy.23.tok_ref = bf16[384,720]{1,0:T(8,128)(2,1)} copy(bf16[384,720]{0,1:T(8,128)(2,1)} %param.13) | data formatting | bytes 1105920 | tf_op args[0]
  7.1 2.1 %copy.24.og_ref = bf16[384,720]{1,0:T(8,128)(2,1)} copy(bf16[384,720]{0,1:T(8,128)(2,1)} %param.14) | data formatting | bytes 1105920 | tf_op args[1]
  9.2 6.5 %copy.18 = bf16[1,2880,720]{2,1,0:T(8,128)(2,1)} copy(bf16[1,2880,720]{1,2,0:T(8,128)(2,1)} %param.18) | data formatting | bytes 8294400 | tf_op args[5]
  15.7 6.5 %copy.19 = bf16[1,2880,720]{2,1,0:T(8,128)(2,1)} copy(bf16[1,2880,720]{1,2,0:T(8,128)(2,1)} %param.19) | data formatting | bytes 8294400 | tf_op args[6]
  22.2 124.7 %exchange.1 = (bf16[4,4,144,768]{3,2,1,0:T(8,128)(2,1)}, bf16[4,4,144,768]{3,2,1,0:T(8,128)(2,1)}, bf16[4,144,768]{2,1,0:T(8,128)(2,1)}, bf16[4,144,768]{2,1,0:T...) custom-call(s32[384,4]{1,0:T(8,128)} %copy.25.ids_ref, s32[128,1]{1,0:T(8,128)} %copy.26.pcol_ref, ...), custom_call_target="tpu_custom_call" | custom-call | tf_op jit(solution)/shard_map/exchange/pallas_call | solution.py:393
  146.9 20.1 %grads.1 = (bf16[384,720]{1,0:T(8,128)(2,1)}, bf16[2880,720]{1,0:T(8,128)(2,1)}, bf16[2880,720]{1,0:T(8,128)(2,1)}, bf16[720,2880]{1,0:T(8,128)(2,1)}, bf16[384,4]{1,0:T(8,128)(2,1)}) custom-call(s32[384,4]{1,0:T(8,128)} %copy.25.ids_ref, s32[128,1]{1,0:T(8,128)} %copy.26.pcol_ref, s32[768,1]{1,0:T(8,128)} %constant.14.clone.c24_ref, ...), custom_call_target="tpu_custom_call" | custom-call | tf_op jit(solution)/shard_map/grads/pallas_call | solution.py:423
  167.0 2.1 %copy.27 = bf16[384,720]{0,1:T(8,128)(2,1)} copy(bf16[384,720]{1,0:T(8,128)(2,1)} %get-tuple-element.27) | data formatting | bytes 1105920
  169.1 0.0 copy-start
  169.1 6.4 %copy.28 = bf16[1,2880,720]{1,2,0:T(8,128)(2,1)} copy(bf16[1,2880,720]{2,1,0:T(8,128)(2,1)} %bitcast.16) | data formatting | bytes 8294400
  175.6 0.0 copy-done
  175.6 0.7 copy.30
  176.3 6.4 %copy.29 = bf16[1,2880,720]{1,2,0:T(8,128)(2,1)} copy(bf16[1,2880,720]{2,1,0:T(8,128)(2,1)} %bitcast.15) | data formatting | bytes 8294400
Async XLA Ops:
  169.1 6.5 %copy-start = (bf16[384,4]{1,0:T(8,128)(2,1)S(1)}, bf16[384,4]{1,0:T(8,128)(2,1)}, u32[]{:S(2)}) copy-start(bf16[384,4]{1,0:T(8,128)(2,1)} %get-tuple-element.31) | copy-start | bytes 9220
where the time goes:
time: 184 us; the launch traced here: 183 us
  Pallas kernels  145 us (79%)
  local copies, waits for them, and re-layouts  37.2 us (20%)
    pallas_call x1, Pallas kernels, shards(): pl.pallas_call(comm_kernel, out_shape=(quart, quart, grp, grp, grp, jax.S...  125 us
    unnamed x12, local copies, waits for them, and re-layouts  35.9 us
    pallas_call x1, Pallas kernels, shards(): pl.pallas_call(grads_kernel, grid=(NT,), out_shape=(jax.ShapeDtypeStruct(...  20.1 us

commit v1 on v0

--- a/solution.py
+++ b/solution.py
@@ -18,6 +18,8 @@
 PL = 8
 G = 4
 GR = PL * CAP
+WR, WCH = 144, 5
+NW = 640
 SRC_ORDER = (0, 1, 3, 2)
 DST_ORDER = (0, 3, 1, 2)
 LANES = (((1,), (1,)), ((), ()))
@@ -36,24 +38,28 @@
     return lax.broadcasted_iota(jnp.int32, shape, dim)
 
 
-def owner_table(pcol):
-    return jnp.where(pcol == 4 * iota((128, 128), 1), 1.0, 0.0).astype(BF16)
+def owner_table(prow):
+    return jnp.where(prow == 4 * iota((128, 128), 0), 1.0, 0.0).astype(BF16)
+
+
+def picks(ids, k):
+    return iota((128, TOK), 0) == ids[k : k + 1, :]
 
 
 def route_ranks(ids, table):
-    hit = jnp.zeros((TOK, 128), F32)
+    hit = jnp.zeros((128, TOK), F32)
     for k in range(4):
-        hit += jnp.where(ids[:, k : k + 1] == iota((TOK, 128), 1), 1.0, 0.0)
-    member = dot(hit.astype(BF16), table)
-    lower = jnp.where(iota((TOK, TOK), 0) > iota((TOK, TOK), 1), 1.0, 0.0).astype(BF16)
-    rank = dot(lower, member.astype(BF16))
+        hit += jnp.where(picks(ids, k), 1.0, 0.0)
+    member = dot(table, hit.astype(BF16))
+    earlier = jnp.where(iota((TOK, TOK), 0) < iota((TOK, TOK), 1), 1.0, 0.0).astype(BF16)
+    rank = dot(member.astype(BF16), earlier)
     return jnp.where(member > 0.5, rank, -1.0).astype(BF16)
 
 
 def comm_kernel(
-    ids_ref, pcol_ref, probs_ref, tok_ref, og_ref, c40_ref, cx_ref, cd_ref, rx_ref, wg_hbm, wu_hbm, wd_hbm,
-    x_out, d_out, dg_out, du_out, pa_out, back_out,
-    send, recv, xb, db, wg, wu, wd, wdq, acc_g, acc_u, acc_d, dg, du, pa, prob, dxs, far_in, left_in, right_in, ret, ret_in,
+    ids_ref, prow_ref, probs_ref, tok_ref, og_ref, c40_ref, cx_ref, cd_ref, rx_ref, wg_hbm, wu_hbm, wd_hbm,
+    x_out, d_out, dgt_out, dut_out, pat_out, back_out,
+    send, recv, xb, db, stage, wq, acc_g, acc_u, acc_d, dg, du, pa, prob, dxs, far_in, left_in, right_in, ret, ret_in, xf, df, dgt, dut, pat,
     w_sem, a2a_s, a2a_r, gat_s, gat_r, far_s, far_r, out_s, left_r, right_r, ret_s, ret_r, o_sem,
 ):
     me = lax.axis_index("dp")
@@ -74,21 +80,24 @@
     for nb in (left, right):
         pl.semaphore_signal(barrier, inc=1, device_id=(me, nb), device_id_type=MESH)
 
-    weights = [
-        pltpu.make_async_copy(src, dst, w_sem.at[i])
-        for i, (src, dst) in enumerate(((wg_hbm, wg), (wu_hbm, wu), (wd_hbm, wd)))
-    ]
-    for w in weights:
-        w.start()
+    weights = (wg_hbm, wu_hbm, wd_hbm)
+
+    def load(n):
+        w, r = n // WCH, n % WCH
+        return pltpu.make_async_copy(
+            weights[w].at[r * WR : (r + 1) * WR], stage.at[n % 3], w_sem.at[n % 3])
+
+    for n in range(3):
+        load(n).start()
 
     ids = ids_ref[...]
-    table = owner_table(pcol_ref[...])
+    table = owner_table(prow_ref[...])
     probs = probs_ref[...].astype(F32)
     ranks = route_ranks(ids, table)
-    pw = jnp.zeros((TOK, 128), F32)
+    pw = jnp.zeros((128, TOK), F32)
     for k in range(4):
-        pw += jnp.where(ids[:, k : k + 1] == iota((TOK, 128), 1), probs[:, k : k + 1], 0.0)
-    owner_p = dot(pw.astype(BF16), table).astype(BF16)
+        pw += jnp.where(picks(ids, k), probs[k : k + 1, :], 0.0)
+    owner_p = dot(table, pw.astype(BF16)).astype(BF16)
 
     def plane(order, i):
         return (z + order[i]) % G
@@ -96,11 +105,11 @@
     def build(zd):
         block, jx, jd = c40_ref[:, 0:1], c40_ref[:, 1:2], c40_ref[:, 2:3]
         mine = iota((PL * SB, 128), 1) == block + zd * PL
-        slots = dot_lanes(jnp.where(mine, 1.0, 0.0).astype(BF16), ranks)
+        slots = dot(jnp.where(mine, 1.0, 0.0).astype(BF16), ranks)
         hot_x = jnp.where(slots == jx.astype(F32), 1.0, 0.0).astype(BF16)
         hot_d = jnp.where(slots == jd.astype(F32), 1.0, 0.0).astype(BF16)
-        rows = dot(hot_x, tok_ref[...]) + dot(hot_d, og_ref[...])
-        p = jnp.sum(jnp.where(mine, dot(hot_x, owner_p), 0.0), axis=1, keepdims=True)
+        rows = dot_lanes(hot_x, tok_ref[...]) + dot_lanes(hot_d, og_ref[...])
+        p = jnp.sum(jnp.where(mine, dot_lanes(hot_x, owner_p), 0.0), axis=1, keepdims=True)
         for j in range(PL):
             part = slice(j * SB, (j + 1) * SB)
             send[zd * PL + j, :, 0:F] = rows[part].astype(BF16)
@@ -136,16 +145,14 @@
             recv[me] = send[me]
         others(zd * PL, lambda o: a2a(o).start())
 
-    for w in weights:
-        w.wait()
-
-    def quarter_rows(r, c):
-        rows = pl.ds(pl.multiple_of(r * 144, 16), 144)
-        for q in range(NT):
-            wdq[q, rows, 0:F] = wd[rows, q * F : (q + 1) * F]
-        return c
-
-    lax.fori_loop(0, F // 144, quarter_rows, 0)
+    def cut(w):
+        for r in range(WCH):
+            n = w * WCH + r
+            load(n).wait()
+            for q in range(NT):
+                wq[w, q, r * WR : (r + 1) * WR, 0:F] = stage[n % 3, :, q * F : (q + 1) * F]
+            if n + 3 < 3 * WCH:
+                load(n + 3).start()
 
     def gat(kind, i, ref, q, to):
         zs = plane(SRC_ORDER, i)
@@ -209,11 +216,10 @@
         acc_d[...] = jnp.zeros_like(acc_d)
 
         def forward(q, c):
-            feats = pl.ds(pl.multiple_of(q * F, 16), F)
             xq = xb[q, zs, :, 0:F]
-            acc_g[...] += dot(xq, wg[feats, :])
-            acc_u[...] += dot(xq, wu[feats, :])
-            acc_d[...] += dot_lanes(db[q, zs, :, 0:F], wdq[q, :, 0:F])
+            acc_g[...] += dot_lanes(xq, wq[0, q, :, 0:F])
+            acc_u[...] += dot_lanes(xq, wq[1, q, :, 0:F])
+            acc_d[...] += dot_lanes(db[q, zs, :, 0:F], wq[2, q, :, 0:F])
             return c
 
         lax.fori_loop(0, NT, forward, 0)
@@ -236,8 +242,7 @@
 
         def backward(r, c):
             q = (t + 2 + r) % NT
-            feats = pl.ds(pl.multiple_of(q * F, 16), F)
-            part = dot_lanes(dg[zs, :, 0:F], wg[feats, :]) + dot_lanes(du[zs, :, 0:F], wu[feats, :])
+            part = dot(dg[zs, :, 0:F], wq[0, q, :, 0:F]) + dot(du[zs, :, 0:F], wq[1, q, :, 0:F])
             dxs[r, zs, :, 0:F] = part.astype(BF16)
             dxs[r, zs, :, F:FP] = prob[:, 0 : FP - F].astype(BF16)
             return c
@@ -281,10 +286,30 @@
             ret_in[me] = ret[me]
         others(zs * PL, lambda s: back(s).start())
 
+    def widen(i):
+        zs = plane(SRC_ORDER, i)
+
+        def body(r, c):
+            rows = pl.ds(pl.multiple_of(r * 48, 16), 48)
+            to = pl.ds(pl.multiple_of(zs * GR + r * 48, 16), 48)
+            for q in range(NT):
+                xf[to, q * F : (q + 1) * F] = xb[q, zs, rows, 0:F]
+                df[to, q * F : (q + 1) * F] = db[q, zs, rows, 0:F]
+            return c
+
+        lax.fori_loop(0, GR // 48, body, 0)
+
+    outs = [
+        pltpu.make_async_copy(src, dst, o_sem.at[i])
+        for i, (src, dst) in enumerate(((xf, x_out), (df, d_out), (dgt, dgt_out), (dut, dut_out), (pat, pat_out)))
+    ]
     stage_d(0)
+    cut(0)
     stage_d(1)
+    cut(1)
     stage_f(0)
     stage_d(2)
+    cut(2)
     stage_f(1)
     stage_d(3)
     stage_f(2)
@@ -292,19 +317,22 @@
     stage_f(3)
     stage_c(1)
     stage_s(0)
+    widen(0)
     stage_c(2)
     stage_s(1)
     stage_e(0)
+    widen(1)
     stage_c(3)
-    outs = [
-        pltpu.make_async_copy(src, dst, o_sem.at[i])
-        for i, (src, dst) in enumerate(((xb, x_out), (db, d_out), (dg, dg_out), (du, du_out), (pa, pa_out)))
-    ]
-    for o in outs:
-        o.start()
     stage_s(2)
     stage_e(1)
+    widen(2)
     stage_s(3)
+    widen(3)
+    outs[0].start()
+    outs[1].start()
+    for i, (src, dst) in enumerate(((dg, dgt), (du, dut), (pa, pat))):
+        dst[...] = src[...].reshape(G * GR, FP)[:, 0:F].T
+        outs[2 + i].start()
     stage_e(2)
     stage_e(3)
 
@@ -330,38 +358,28 @@
 
 
 def grads_kernel(
-    ids_ref, pcol_ref, c24_ref, x_ref, d_ref, dg_ref, du_ref, pa_ref, back_ref,
+    ids_ref, prow_ref, c24_ref, x_ref, d_ref, dgt_ref, dut_ref, pat_ref, back_ref,
     in_grad, gate_grad, up_grad, down_grad, prob_grad,
 ):
-    q = pl.program_id(0)
-    xq = x_ref[0, :, 0:F]
-    xt = xq.T
-    gate_grad[...] = dot(xt, dg_ref[:, 0:F]).astype(BF16)
-    up_grad[...] = dot(xt, du_ref[:, 0:F]).astype(BF16)
-    pt = pa_ref[:, 0:F].T
-    piece = dot(pt, d_ref[0, :, 0:F]).astype(BF16)
-    for k in range(NT):
-
-        @pl.when(q == k)
-        def _():
-            down_grad[:, k * F : (k + 1) * F] = piece
-
-    @pl.when(q == 0)
+    x = x_ref[...]
+    gate_grad[...] = dot(dgt_ref[...], x).astype(BF16)
+    up_grad[...] = dot(dut_ref[...], x).astype(BF16)
+    down_grad[...] = dot(pat_ref[...], d_ref[...]).astype(BF16)
+
+    @pl.when(pl.program_id(0) == 0)
     def _():
         ids = ids_ref[...]
-        table = owner_table(pcol_ref[...])
+        table = owner_table(prow_ref[...])
         ranks = route_ranks(ids, table)
-        spread = jnp.where(iota((NDP * RB, 128), 1) == c24_ref[...], 1.0, 0.0).astype(BF16)
-        slots = dot_lanes(ranks, spread)
-        row = lax.broadcasted_iota(jnp.int32, (TOK, NDP * RB), 1)
-        hot = jnp.where(slots == (row % RB).astype(F32), 1.0, 0.0).astype(BF16)
-        sums = dot(hot, back_ref[:, 0:F])
-        in_grad[...] = sums.astype(BF16)
-        ones = dot(hot, jnp.where(iota((NDP * RB, 128), 1) == c24_ref[...], back_ref[:, FP - 128 :][:, 127:128].astype(F32), 0.0).astype(BF16))
+        mine = iota((NDP * RB, 128), 1) == c24_ref[:, 0:1]
+        slots = dot(jnp.where(mine, 1.0, 0.0).astype(BF16), ranks)
+        hot = jnp.where(slots == c24_ref[:, 1:2].astype(F32), 1.0, 0.0).astype(BF16)
+        in_grad[...] = dot(back_ref[:, 0:F].T, hot).astype(BF16)
+        prob = jnp.where(mine, back_ref[:, FP - 128 :][:, 127:128].astype(F32), 0.0).astype(BF16)
+        by_owner = dot(prob.T, hot)
         for k in range(4):
-            pick = jnp.where(ids[:, k : k + 1] == iota((TOK, 128), 1), 1.0, 0.0).astype(BF16)
-            mine = dot(pick, table)
-            prob_grad[:, k : k + 1] = jnp.sum(mine * ones, axis=1, keepdims=True).astype(BF16)
+            owner = dot(table, jnp.where(picks(ids, k), 1.0, 0.0).astype(BF16))
+            prob_grad[k : k + 1, :] = jnp.sum(owner * by_owner, axis=0, keepdims=True).astype(BF16)
 
 
 def tables():
@@ -378,34 +396,36 @@
             cx[j * CAP + k, j * SB + k] = 1
             cd[j * CAP + k, j * SB + DOFF + k] = 1
             rx[j * RB + k, j * CAP + k] = 1
-    c24 = (np.arange(NDP * RB) // RB).astype(np.int32)[:, None]
+    r = np.arange(NDP * RB)
+    c24 = np.stack([r // RB, r % RB], axis=1).astype(np.int32)
     return c40, cx, cd, rx, c24
 
 
 def shards(tokens, out_grad, route_probs, expert_ids, placement_map, w_gate, w_up, w_down):
     c40, cx, cd, rx, c24 = tables()
-    pcol = placement_map[:, None]
+    ids, prow = expert_ids.T, placement_map[None, :]
     vmem = pl.BlockSpec(memory_space=pltpu.VMEM)
     hbm = pl.BlockSpec(memory_space=pl.ANY)
-    grp = jax.ShapeDtypeStruct((G, GR, FP), BF16)
-    quart = jax.ShapeDtypeStruct((NT, G, GR, FP), BF16)
+    turned = jax.ShapeDtypeStruct((F, G * GR), BF16)
+    wide = jax.ShapeDtypeStruct((G * GR, NT * F), BF16)
     dma = pltpu.SemaphoreType.DMA
-    x, d, dg, du, pa, back = pl.pallas_call(
+    x, d, dgt, dut, pat, back = pl.pallas_call(
         comm_kernel,
-        out_shape=(quart, quart, grp, grp, grp, jax.ShapeDtypeStruct((NDP, RB, FP), BF16)),
+        out_shape=(wide, wide, turned, turned, turned, jax.ShapeDtypeStruct((NDP, RB, FP), BF16)),
         in_specs=[vmem] * 9 + [hbm] * 3,
         out_specs=[hbm] * 6,
         scratch_shapes=[
             pltpu.VMEM((NDP, SB, FP), BF16), pltpu.VMEM((NDP, SB, FP), BF16),
             pltpu.VMEM((NT, G, GR, FP), BF16), pltpu.VMEM((NT, G, GR, FP), BF16),
-            pltpu.VMEM((NT * F, F), BF16), pltpu.VMEM((NT * F, F), BF16), pltpu.VMEM((F, NT * F), BF16),
-            pltpu.VMEM((NT, F, FP), BF16),
+            pltpu.VMEM((3, WR, NT * F), BF16), pltpu.VMEM((3, NT, F, FP), BF16),
             pltpu.VMEM((GR, F), F32), pltpu.VMEM((GR, F), F32), pltpu.VMEM((GR, F), F32),
             pltpu.VMEM((G, GR, FP), BF16), pltpu.VMEM((G, GR, FP), BF16), pltpu.VMEM((G, GR, FP), BF16),
             pltpu.VMEM((GR, 128), F32),
             pltpu.VMEM((NT, G, GR, FP), BF16),
             pltpu.VMEM((G, GR, FP), BF16), pltpu.VMEM((G, GR, FP), BF16), pltpu.VMEM((G, GR, FP), BF16),
             pltpu.VMEM((NDP, RB, FP), BF16), pltpu.VMEM((NDP, RB, FP), BF16),
+            pltpu.VMEM((G * GR, NT * F), BF16), pltpu.VMEM((G * GR, NT * F), BF16),
+            pltpu.VMEM((F, G * GR), BF16), pltpu.VMEM((F, G * GR), BF16), pltpu.VMEM((F, G * GR), BF16),
             dma((3,)), dma((NDP,)), dma((NDP,)), dma((6, G)), dma((6, G)), dma((G,)), dma((G,)),
             dma((2, G)), dma((G,)), dma((G,)), dma((NDP,)), dma((NDP,)), dma((6,)),
         ],
@@ -414,42 +434,29 @@
         ),
         name="exchange",
     )(
-        expert_ids, pcol, route_probs, tokens, out_grad,
+        ids, prow, route_probs.T, tokens.T, out_grad.T,
         jnp.asarray(c40), jnp.asarray(cx, BF16), jnp.asarray(cd, BF16), jnp.asarray(rx, BF16),
-        w_gate[0], w_up[0], w_down[0],
+        w_gate[0].T, w_up[0].T, w_down[0],
     )
     rows = G * GR
-    whole = lambda *s: pl.BlockSpec(s, lambda q: (0,) * len(s))
+    whole = lambda *s: pl.BlockSpec(s, lambda n: (0,) * len(s))
+    strip = lambda r: pl.BlockSpec((r, NW), lambda n: (0, n))
+    grad = jax.ShapeDtypeStruct((F, NT * F), BF16)
     in_grad, gate_grad, up_grad, down_grad, prob_grad = pl.pallas_call(
         grads_kernel,
-        grid=(NT,),
+        grid=(-(-NT * F // NW),),
         out_shape=(
-            jax.ShapeDtypeStruct((TOK, F), BF16),
-            jax.ShapeDtypeStruct((NT * F, F), BF16),
-            jax.ShapeDtypeStruct((NT * F, F), BF16),
-            jax.ShapeDtypeStruct((F, NT * F), BF16),
-            jax.ShapeDtypeStruct((TOK, 4), BF16),
+            jax.ShapeDtypeStruct((F, TOK), BF16), grad, grad, grad, jax.ShapeDtypeStruct((4, TOK), BF16),
         ),
         in_specs=[
-            whole(TOK, 4), whole(128, 1), whole(NDP * RB, 1),
-            pl.BlockSpec((1, rows, FP), lambda q: (q, 0, 0)), pl.BlockSpec((1, rows, FP), lambda q: (q, 0, 0)),
-            whole(rows, FP), whole(rows, FP), whole(rows, FP), whole(NDP * RB, FP),
+            whole(4, TOK), whole(1, 128), whole(NDP * RB, 2), strip(rows), strip(rows),
+            whole(F, rows), whole(F, rows), whole(F, rows), whole(NDP * RB, FP),
         ],
-        out_specs=[
-            whole(TOK, F),
-            pl.BlockSpec((F, F), lambda q: (q, 0)),
-            pl.BlockSpec((F, F), lambda q: (q, 0)),
-            whole(F, NT * F),
-            whole(TOK, 4),
-        ],
+        out_specs=[whole(F, TOK), strip(F), strip(F), strip(F), whole(4, TOK)],
         compiler_params=pltpu.CompilerParams(vmem_limit_bytes=60 * 1024 * 1024),
         name="grads",
-    )(
-        expert_ids, pcol, jnp.asarray(c24),
-        x.reshape(NT, rows, FP), d.reshape(NT, rows, FP),
-        dg.reshape(rows, FP), du.reshape(rows, FP), pa.reshape(rows, FP), back.reshape(NDP * RB, FP),
-    )
-    return (in_grad, gate_grad[None], up_grad[None], down_grad[None], prob_grad)
+    )(ids, prow, jnp.asarray(c24), x, d, dgt, dut, pat, back.reshape(NDP * RB, FP))
+    return (in_grad.T, gate_grad.T[None], up_grad.T[None], down_grad[None], prob_grad.T)
 
 
 def solution(mesh):

time: 184 us -> 146 us (0.79)
  local copies, waits for them, and re-layouts: 37.2 us -> 0 us
    unnamed x12 -> x0, local copies, waits for them, and re-layouts: 35.9 us -> none
where the time goes in v1:
time: 146 us
  Pallas kernels  145 us (99%)
    pallas_call x1, Pallas kernels, shards(): pl.pallas_call(comm_kernel, out_shape=(wide, wide, turned, turned, turned...  125 us
    pallas_call x1, Pallas kernels, shards(): pl.pallas_call(grads_kernel, grid=(-(-NT * F // NW),), out_shape=(jax.Sha...  19.8 us

profile of v1, /device:TPU:1, one launch (start us, length us, event | category | flops | bytes accessed | tf_op | source)
XLA Modules:
  0.0 145.5 jit_solution(2287151232456482682)
XLA Ops:
  0.6 125.0 %exchange.1 = (bf16[576,2880]{1,0:T(8,128)(2,1)}, bf16[576,2880]{1,0:T(8,128)(2,1)}, bf16[720,576]{1,0:T(8,128)(2,1)}, bf16[720,576]{1,0:T(8,128)(2,1)}, bf16[72...) custom-call(s32[4,384]{1,0:T(4,128)} %bitcast.28, s32[1,128]{1,0:T(1,128)} %bitcast.31, bf16[4,384]{1,0:T(4,128)(2,1)} %bitcast.30, ...), custom_call_target="tpu_custom_call" | custom-call | tf_op jit(solution)/shard_map/exchange/pallas_call | solution.py:412
  125.6 19.8 %grads.1 = (bf16[720,384]{1,0:T(8,128)(2,1)}, bf16[720,2880]{1,0:T(8,128)(2,1)}, bf16[720,2880]{1,0:T(8,128)(2,1)}, bf16[720,2880]{1,0:T(8,128)(2,1)}, bf16[4,384]{1,0:T(4,128)(2,1)}) custom-call(s32[4,384]{1,0:T(4,128)} %bitcast.29, s32[1,128]{1,0:T(1,128)} %bitcast.32, s32[768,2]{1,0:T(8,128)} %constant.14.clone.c24_ref, ...), custom_call_target="tpu_custom_call" | custom-call | tf_op jit(solution)/shard_map/grads/pallas_call | solution.py:445

commit v2 on v1

--- a/solution.py
+++ b/solution.py
@@ -19,7 +19,7 @@
 G = 4
 GR = PL * CAP
 WR, WCH = 144, 5
-NW = 640
+EXCHANGE_VMEM, COMBINE_VMEM = 48 * 2**20, 16 * 2**20
 SRC_ORDER = (0, 1, 3, 2)
 DST_ORDER = (0, 3, 1, 2)
 LANES = (((1,), (1,)), ((), ()))
@@ -58,14 +58,17 @@
 
 def comm_kernel(
     ids_ref, prow_ref, probs_ref, tok_ref, og_ref, c40_ref, cx_ref, cd_ref, rx_ref, wg_hbm, wu_hbm, wd_hbm,
-    x_out, d_out, dgt_out, dut_out, pat_out, back_out,
-    send, recv, xb, db, stage, wq, acc_g, acc_u, acc_d, dg, du, pa, prob, dxs, far_in, left_in, right_in, ret, ret_in, xf, df, dgt, dut, pat,
-    w_sem, a2a_s, a2a_r, gat_s, gat_r, far_s, far_r, out_s, left_r, right_r, ret_s, ret_r, o_sem,
+    grads, back_out,
+    send, recv, xd, stage, wq, acc_g, acc_u, acc_d, fac, prob, dxs, far_in, left_in, right_in, ret, ret_in, turned,
+    w_sem, a2a_s, a2a_r, gat_s, gat_r, far_s, far_r, out_s, left_r, right_r, ret_s, ret_r,
 ):
     me = lax.axis_index("dp")
     t = lax.axis_index("tensor")
     z = me // PL
     right, left, far = (t + 1) % NT, (t + 3) % NT, (t + 2) % NT
+
+    xb, db = xd.at[0], xd.at[1]
+    dg, du, pa = fac.at[0], fac.at[1], fac.at[2]
 
     barrier = pltpu.get_barrier_semaphore()
 
@@ -286,55 +289,52 @@
             ret_in[me] = ret[me]
         others(zs * PL, lambda s: back(s).start())
 
-    def widen(i):
-        zs = plane(SRC_ORDER, i)
-
-        def body(r, c):
-            rows = pl.ds(pl.multiple_of(r * 48, 16), 48)
-            to = pl.ds(pl.multiple_of(zs * GR + r * 48, 16), 48)
-            for q in range(NT):
-                xf[to, q * F : (q + 1) * F] = xb[q, zs, rows, 0:F]
-                df[to, q * F : (q + 1) * F] = db[q, zs, rows, 0:F]
-            return c
-
-        lax.fori_loop(0, GR // 48, body, 0)
-
-    outs = [
-        pltpu.make_async_copy(src, dst, o_sem.at[i])
-        for i, (src, dst) in enumerate(((xf, x_out), (df, d_out), (dgt, dgt_out), (dut, dut_out), (pat, pat_out)))
-    ]
+    def turn(w):
+        turned[w] = fac[w].reshape(G * GR, FP)[:, 0:F].T
+
+    def grad(w, quarters):
+        for q in quarters:
+            rows = xd[w // 2, q].reshape(G * GR, FP)[:, 0:F]
+            grads[w, :, q * F : (q + 1) * F] = dot(turned[w], rows).astype(BF16)
+
     stage_d(0)
+    stage_d(1)
     cut(0)
-    stage_d(1)
-    cut(1)
     stage_f(0)
     stage_d(2)
+    stage_f(1)
+    cut(1)
+    stage_d(3)
     cut(2)
-    stage_f(1)
-    stage_d(3)
+    stage_c(0)
     stage_f(2)
-    stage_c(0)
+    stage_c(1)
     stage_f(3)
-    stage_c(1)
     stage_s(0)
-    widen(0)
     stage_c(2)
     stage_s(1)
+    stage_c(3)
     stage_e(0)
-    widen(1)
-    stage_c(3)
     stage_s(2)
     stage_e(1)
-    widen(2)
+    turn(0)
+    grad(0, (0,))
+    grad(0, (1,))
+    turn(1)
     stage_s(3)
-    widen(3)
-    outs[0].start()
-    outs[1].start()
-    for i, (src, dst) in enumerate(((dg, dgt), (du, dut), (pa, pat))):
-        dst[...] = src[...].reshape(G * GR, FP)[:, 0:F].T
-        outs[2 + i].start()
+    grad(0, (2,))
+    grad(0, (3,))
+    grad(1, (0,))
     stage_e(2)
+    turn(2)
+    grad(1, (1,))
     stage_e(3)
+    grad(1, (2,))
+    grad(1, (3,))
+    grad(2, (0,))
+    grad(2, (1,))
+    grad(2, (2,))
+    grad(2, (3,))
 
     for i in range(G):
         for kind in range(6):
@@ -350,36 +350,36 @@
         return c
 
     lax.fori_loop(0, NDP, finish, 0)
-    for o in outs:
-        o.wait()
-    last = pltpu.make_async_copy(ret_in, back_out, o_sem.at[5])
-    last.start()
-    last.wait()
-
-
-def grads_kernel(
-    ids_ref, prow_ref, c24_ref, x_ref, d_ref, dgt_ref, dut_ref, pat_ref, back_ref,
-    in_grad, gate_grad, up_grad, down_grad, prob_grad,
+
+    def hand_on(o, c):
+        back_out[o] = ret_in[o]
+        return c
+
+    lax.fori_loop(0, NDP, hand_on, 0)
+
+
+def combine_kernel(
+    ids_ref, prow_ref, c24_ref, back_ref, grads, in_grad, gate_grad, up_grad, down_grad, prob_grad, sem
 ):
-    x = x_ref[...]
-    gate_grad[...] = dot(dgt_ref[...], x).astype(BF16)
-    up_grad[...] = dot(dut_ref[...], x).astype(BF16)
-    down_grad[...] = dot(pat_ref[...], d_ref[...]).astype(BF16)
-
-    @pl.when(pl.program_id(0) == 0)
-    def _():
-        ids = ids_ref[...]
-        table = owner_table(prow_ref[...])
-        ranks = route_ranks(ids, table)
-        mine = iota((NDP * RB, 128), 1) == c24_ref[:, 0:1]
-        slots = dot(jnp.where(mine, 1.0, 0.0).astype(BF16), ranks)
-        hot = jnp.where(slots == c24_ref[:, 1:2].astype(F32), 1.0, 0.0).astype(BF16)
-        in_grad[...] = dot(back_ref[:, 0:F].T, hot).astype(BF16)
-        prob = jnp.where(mine, back_ref[:, FP - 128 :][:, 127:128].astype(F32), 0.0).astype(BF16)
-        by_owner = dot(prob.T, hot)
-        for k in range(4):
-            owner = dot(table, jnp.where(picks(ids, k), 1.0, 0.0).astype(BF16))
-            prob_grad[k : k + 1, :] = jnp.sum(owner * by_owner, axis=0, keepdims=True).astype(BF16)
+    writes = [
+        pltpu.make_async_copy(grads.at[w], dst, sem.at[w]) for w, dst in enumerate((gate_grad, up_grad, down_grad))
+    ]
+    for w in writes:
+        w.start()
+    ids = ids_ref[...]
+    table = owner_table(prow_ref[...])
+    ranks = route_ranks(ids, table)
+    mine = iota((NDP * RB, 128), 1) == c24_ref[:, 0:1]
+    slots = dot(jnp.where(mine, 1.0, 0.0).astype(BF16), ranks)
+    hot = jnp.where(slots == c24_ref[:, 1:2].astype(F32), 1.0, 0.0).astype(BF16)
+    in_grad[...] = dot(back_ref[:, 0:F].T, hot).astype(BF16)
+    prob = jnp.where(mine, back_ref[:, FP - 128 :][:, 127:128].astype(F32), 0.0).astype(BF16)
+    by_owner = dot(prob.T, hot)
+    for k in range(4):
+        owner = dot(table, jnp.where(picks(ids, k), 1.0, 0.0).astype(BF16))
+        prob_grad[k : k + 1, :] = jnp.sum(owner * by_owner, axis=0, keepdims=True).astype(BF16)
+    for w in writes:
+        w.wait()
 
 
 def tables():
@@ -407,30 +407,28 @@
     vmem = pl.BlockSpec(memory_space=pltpu.VMEM)
     hbm = pl.BlockSpec(memory_space=pl.ANY)
     turned = jax.ShapeDtypeStruct((F, G * GR), BF16)
-    wide = jax.ShapeDtypeStruct((G * GR, NT * F), BF16)
     dma = pltpu.SemaphoreType.DMA
-    x, d, dgt, dut, pat, back = pl.pallas_call(
+    grads, back = pl.pallas_call(
         comm_kernel,
-        out_shape=(wide, wide, turned, turned, turned, jax.ShapeDtypeStruct((NDP, RB, FP), BF16)),
+        out_shape=(pltpu.VMEM((3, F, NT * F), BF16), pltpu.VMEM((NDP, RB, FP), BF16)),
         in_specs=[vmem] * 9 + [hbm] * 3,
-        out_specs=[hbm] * 6,
+        out_specs=[vmem, vmem],
         scratch_shapes=[
             pltpu.VMEM((NDP, SB, FP), BF16), pltpu.VMEM((NDP, SB, FP), BF16),
-            pltpu.VMEM((NT, G, GR, FP), BF16), pltpu.VMEM((NT, G, GR, FP), BF16),
+            pltpu.VMEM((2, NT, G, GR, FP), BF16),
             pltpu.VMEM((3, WR, NT * F), BF16), pltpu.VMEM((3, NT, F, FP), BF16),
             pltpu.VMEM((GR, F), F32), pltpu.VMEM((GR, F), F32), pltpu.VMEM((GR, F), F32),
-            pltpu.VMEM((G, GR, FP), BF16), pltpu.VMEM((G, GR, FP), BF16), pltpu.VMEM((G, GR, FP), BF16),
+            pltpu.VMEM((3, G, GR, FP), BF16),
             pltpu.VMEM((GR, 128), F32),
             pltpu.VMEM((NT, G, GR, FP), BF16),
             pltpu.VMEM((G, GR, FP), BF16), pltpu.VMEM((G, GR, FP), BF16), pltpu.VMEM((G, GR, FP), BF16),
             pltpu.VMEM((NDP, RB, FP), BF16), pltpu.VMEM((NDP, RB, FP), BF16),
-            pltpu.VMEM((G * GR, NT * F), BF16), pltpu.VMEM((G * GR, NT * F), BF16),
-            pltpu.VMEM((F, G * GR), BF16), pltpu.VMEM((F, G * GR), BF16), pltpu.VMEM((F, G * GR), BF16),
+            pltpu.VMEM((3, F, G * GR), BF16),
             dma((3,)), dma((NDP,)), dma((NDP,)), dma((6, G)), dma((6, G)), dma((G,)), dma((G,)),
-            dma((2, G)), dma((G,)), dma((G,)), dma((NDP,)), dma((NDP,)), dma((6,)),
+            dma((2, G)), dma((G,)), dma((G,)), dma((NDP,)), dma((NDP,)),
         ],
         compiler_params=pltpu.CompilerParams(
-            collective_id=0, has_side_effects=True, vmem_limit_bytes=60 * 1024 * 1024
+            collective_id=0, has_side_effects=True, vmem_limit_bytes=EXCHANGE_VMEM
         ),
         name="exchange",
     )(
@@ -438,24 +436,18 @@
         jnp.asarray(c40), jnp.asarray(cx, BF16), jnp.asarray(cd, BF16), jnp.asarray(rx, BF16),
         w_gate[0].T, w_up[0].T, w_down[0],
     )
-    rows = G * GR
-    whole = lambda *s: pl.BlockSpec(s, lambda n: (0,) * len(s))
-    strip = lambda r: pl.BlockSpec((r, NW), lambda n: (0, n))
     grad = jax.ShapeDtypeStruct((F, NT * F), BF16)
     in_grad, gate_grad, up_grad, down_grad, prob_grad = pl.pallas_call(
-        grads_kernel,
-        grid=(-(-NT * F // NW),),
+        combine_kernel,
         out_shape=(
             jax.ShapeDtypeStruct((F, TOK), BF16), grad, grad, grad, jax.ShapeDtypeStruct((4, TOK), BF16),
         ),
-        in_specs=[
-            whole(4, TOK), whole(1, 128), whole(NDP * RB, 2), strip(rows), strip(rows),
-            whole(F, rows), whole(F, rows), whole(F, rows), whole(NDP * RB, FP),
-        ],
-        out_specs=[whole(F, TOK), strip(F), strip(F), strip(F), whole(4, TOK)],
-        compiler_params=pltpu.CompilerParams(vmem_limit_bytes=60 * 1024 * 1024),
-        name="grads",
-    )(ids, prow, jnp.asarray(c24), x, d, dgt, dut, pat, back.reshape(NDP * RB, FP))
+        in_specs=[vmem] * 5,
+        out_specs=[vmem, hbm, hbm, hbm, vmem],
+        scratch_shapes=[dma((3,))],
+        compiler_params=pltpu.CompilerParams(vmem_limit_bytes=COMBINE_VMEM),
+        name="combine",
+    )(ids, prow, jnp.asarray(c24), back.reshape(NDP * RB, FP), grads)
     return (in_grad.T, gate_grad.T[None], up_grad.T[None], down_grad[None], prob_grad.T)
 
 

time: 146 us -> 126 us (0.86)
  Pallas kernels: 145 us -> 125 us
    pallas_call x2, Pallas kernels: 145 us -> 125 us  [the longest x1 119 us: shards(): pl.pallas_call(comm_kernel, out_shape=(pltpu.VMEM((3, F, NT * F), BF16),...]
where the time goes in v2:
time: 126 us; the launch traced here: 125 us
  Pallas kernels  125 us (99%)
    pallas_call x1, Pallas kernels, shards(): pl.pallas_call(comm_kernel, out_shape=(pltpu.VMEM((3, F, NT * F), BF16),...  119 us
    pallas_call x1, Pallas kernels, shards(): pl.pallas_call(combine_kernel, out_shape=(jax.ShapeDtypeStruct((F, TOK),...  5.66 us

profile of v2, /device:TPU:1, one launch (start us, length us, event | category | flops | bytes accessed | tf_op | source)
XLA Modules:
  0.0 125.4 jit_solution(14397552274109343115)
XLA Ops:
  0.6 0.0 copy-start
  0.6 0.0 copy-start.1
  0.7 0.0 copy-start.2
  0.7 118.9 %exchange.1 = (bf16[3,720,2880]{2,1,0:T(8,128)(2,1)S(1)}, bf16[32,24,768]{2,1,0:T(8,128)(2,1)S(1)}) custom-call(s32[4,384]{1,0:T(4,128)} %bitcast.23, s32[1,128]{1,0:T(1,128)} %bitcast.25, bf16[4,384]{1,0:T(4,128)(2,1)} %bitcast.32, bf16[720,384]{1,0:T(8,128)(2,1)} %bitcast.30, bf16[720,384]{1,0:T(8,128)(2,1)} %bitcast.31, s32[320,3]{1,0:T(8,128)} %constant.10.clone.c40_ref, ...), custom_call_target="tpu_custom_call" | custom-call | tf_op jit(solution)/shard_map/exchange/pallas_call | solution.py:411
  119.6 0.0 copy-done
  119.6 0.0 copy-done.1
  119.6 0.0 copy-done.2
  119.6 5.7 %combine.1 = (bf16[720,384]{1,0:T(8,128)(2,1)}, bf16[720,2880]{1,0:T(8,128)(2,1)}, bf16[720,2880]{1,0:T(8,128)(2,1)}, bf16[720,2880]{1,0:T(8,128)(2,1)}, bf16[4,384]{1,0:T(4,128)(2,1)}) custom-call(s32[4,384]{1,0:T(4,128)S(1)} %bitcast.24, s32[1,128]{1,0:T(1,128)S(1)} %bitcast.26, s32[768,2]{1,0:T(8,128)S(1)} %copy-done, bf16[768,768]{1,0:T(8,128)(2,1)S(1)} %bitcast.22, ...), custom_call_target="tpu_custom_call" | custom-call | tf_op jit(solution)/shard_map/combine/pallas_call | solution.py:440
Async XLA Ops:
  0.6 118.9 %copy-start = (s32[768,2]{1,0:T(8,128)S(1)}, s32[768,2]{1,0:T(8,128)}, u32[]{:S(2)}) copy-start(s32[768,2]{1,0:T(8,128)} %constant.14.clone.c24_ref) | copy-start | bytes 18436
  0.6 118.9 %copy-start.1 = (s32[384,4]{0,1:T(4,128)S(1)}, s32[384,4]{0,1:T(4,128)}, u32[]{:S(2)}) copy-start(s32[384,4]{0,1:T(4,128)} %param.16) | copy-start | bytes 18436
  0.7 118.9 %copy-start.2 = (s32[128]{0:T(128)S(1)}, s32[128]{0:T(128)}, u32[]{:S(2)}) copy-start(s32[128]{0:T(128)} %param.17) | copy-start | bytes 1540

commit v3 on v2

--- a/solution.py
+++ b/solution.py
@@ -20,8 +20,12 @@
 GR = PL * CAP
 WR, WCH = 144, 5
 EXCHANGE_VMEM, COMBINE_VMEM = 48 * 2**20, 16 * 2**20
-SRC_ORDER = (0, 1, 3, 2)
-DST_ORDER = (0, 3, 1, 2)
+NEAR = (
+    ((0, 0), (0, 1), (0, 3), (1, 0)),
+    ((1, 1), (1, 3), (3, 1), (3, 3)),
+    ((2, 1), (2, 3), (1, 2), (3, 2)),
+    ((2, 2), (0, 2), (2, 0), (3, 0)),
+)
 LANES = (((1,), (1,)), ((), ()))
 F32, BF16 = jnp.float32, jnp.bfloat16
 
@@ -64,7 +68,7 @@
 ):
     me = lax.axis_index("dp")
     t = lax.axis_index("tensor")
-    z = me // PL
+    z, y, core = me // 8, me // 2 % 4, me % 2
     right, left, far = (t + 1) % NT, (t + 3) % NT, (t + 2) % NT
 
     xb, db = xd.at[0], xd.at[1]
@@ -102,12 +106,30 @@
         pw += jnp.where(picks(ids, k), probs[k : k + 1, :], 0.0)
     owner_p = dot(table, pw.astype(BF16)).astype(BF16)
 
-    def plane(order, i):
-        return (z + order[i]) % G
-
-    def build(zd):
-        block, jx, jd = c40_ref[:, 0:1], c40_ref[:, 1:2], c40_ref[:, 2:3]
-        mine = iota((PL * SB, 128), 1) == block + zd * PL
+    def source(i, j):
+        dz, dy = NEAR[i][j // 2]
+        return (z + dz) % 4 * 8 + (y + dy) % 4 * 2 + j % 2
+
+    def dest(i, j):
+        dz, dy = NEAR[i][j // 2]
+        return (z + 4 - dz) % 4 * 8 + (y + 4 - dy) % 4 * 2 + j % 2
+
+    def others(i, act):
+        for j in range(PL):
+            if i == 0 and j < 2:
+                pl.when(core != j)(functools.partial(act, j))
+            else:
+                act(j)
+
+    def own(at):
+        for j in range(2):
+            pl.when(core == j)(functools.partial(at, j))
+
+    def build(i):
+        jx, jd = c40_ref[:, 0:1], c40_ref[:, 1:2]
+        dz, dy, cores = (c40_ref[:, 2 + 3 * i + k : 3 + 3 * i + k] for k in range(3))
+        block = ((z - dz) & 3) * 8 + ((y - dy) & 3) * 2 + cores
+        mine = iota((PL * SB, 128), 1) == block
         slots = dot(jnp.where(mine, 1.0, 0.0).astype(BF16), ranks)
         hot_x = jnp.where(slots == jx.astype(F32), 1.0, 0.0).astype(BF16)
         hot_d = jnp.where(slots == jd.astype(F32), 1.0, 0.0).astype(BF16)
@@ -115,38 +137,31 @@
         p = jnp.sum(jnp.where(mine, dot_lanes(hot_x, owner_p), 0.0), axis=1, keepdims=True)
         for j in range(PL):
             part = slice(j * SB, (j + 1) * SB)
-            send[zd * PL + j, :, 0:F] = rows[part].astype(BF16)
-            send[zd * PL + j, :, F:FP] = jnp.broadcast_to(p[part], (SB, FP - F)).astype(BF16)
-
-    def a2a(o):
-        return pltpu.make_async_remote_copy(
-            src_ref=send.at[o], dst_ref=recv.at[me], send_sem=a2a_s.at[o], recv_sem=a2a_r.at[me],
-            device_id=(o, t), device_id_type=MESH)
-
-    def a2a_in(s):
-        return pltpu.make_async_remote_copy(
-            src_ref=send.at[s], dst_ref=recv.at[s], send_sem=a2a_s.at[s], recv_sem=a2a_r.at[s],
-            device_id=(s, t), device_id_type=MESH)
-
-    def others(first, act):
-        def body(j, c):
-            o = first + j
-
-            @pl.when(o != me)
-            def _():
-                act(o)
-
-            return c
-
-        lax.fori_loop(0, PL, body, 0)
-
-    for i in range(G):
-        zd = plane(DST_ORDER, i)
-        build(zd)
+            send[i * PL + j, :, 0:F] = rows[part].astype(BF16)
+            send[i * PL + j, :, F:FP] = jnp.broadcast_to(p[part], (SB, FP - F)).astype(BF16)
+
+    def a2a(i, j):
+        return pltpu.make_async_remote_copy(
+            src_ref=send.at[i * PL + j], dst_ref=recv.at[i * PL + j // 2 * 2 + core],
+            send_sem=a2a_s.at[i * PL + j], recv_sem=a2a_r.at[i * PL + j // 2 * 2 + core],
+            device_id=(dest(i, j), t), device_id_type=MESH)
+
+    def a2a_in(i, j):
+        return pltpu.make_async_remote_copy(
+            src_ref=send.at[i * PL + j], dst_ref=recv.at[i * PL + j],
+            send_sem=a2a_s.at[i * PL + j], recv_sem=a2a_r.at[i * PL + j],
+            device_id=(source(i, j), t), device_id_type=MESH)
+
+    def stage_b(i):
+        build(i)
         if i == 0:
             pl.semaphore_wait(barrier, NDP - 1 + 2)
-            recv[me] = send[me]
-        others(zd * PL, lambda o: a2a(o).start())
+
+            def keep(j):
+                recv[j] = send[j]
+
+            own(keep)
+        others(i, lambda j: a2a(i, j).start())
 
     def cut(w):
         for r in range(WCH):
@@ -158,7 +173,7 @@
                 load(n + 3).start()
 
     def gat(kind, i, ref, q, to):
-        zs = plane(SRC_ORDER, i)
+        zs = i
         return pltpu.make_async_remote_copy(
             src_ref=ref.at[q, zs], dst_ref=ref.at[q, zs], send_sem=gat_s.at[kind, i], recv_sem=gat_r.at[kind, i],
             device_id=(me, to), device_id_type=MESH)
@@ -178,9 +193,9 @@
         )[kind]()
 
     def stage_d(i):
-        zs = plane(SRC_ORDER, i)
-        others(zs * PL, lambda s: a2a_in(s).wait_recv())
-        got = recv[pl.ds(zs * PL, PL)].reshape(PL * SB, FP)
+        zs = i
+        others(i, lambda j: a2a_in(i, j).wait_recv())
+        got = recv[i * PL : (i + 1) * PL].reshape(PL * SB, FP)
         xb[t, zs] = dot(cx_ref[...], got).astype(BF16)
         db[t, zs] = dot(cd_ref[...], got).astype(BF16)
         for kind in range(4):
@@ -193,25 +208,25 @@
         gat_out(5, i).start()
 
     def rs_far(i):
-        zs = plane(SRC_ORDER, i)
+        zs = i
         return pltpu.make_async_remote_copy(
             src_ref=dxs.at[0, zs], dst_ref=far_in.at[zs], send_sem=far_s.at[i], recv_sem=far_r.at[i],
             device_id=(me, left if i % 2 == 0 else right), device_id_type=MESH)
 
     def rs_left(i):
-        zs = plane(SRC_ORDER, i)
+        zs = i
         return pltpu.make_async_remote_copy(
             src_ref=dxs.at[1, zs], dst_ref=right_in.at[zs], send_sem=out_s.at[0, i], recv_sem=right_r.at[i],
             device_id=(me, left), device_id_type=MESH)
 
     def rs_right(i):
-        zs = plane(SRC_ORDER, i)
+        zs = i
         return pltpu.make_async_remote_copy(
             src_ref=dxs.at[3, zs], dst_ref=left_in.at[zs], send_sem=out_s.at[1, i], recv_sem=left_r.at[i],
             device_id=(me, right), device_id_type=MESH)
 
     def stage_c(i):
-        zs = plane(SRC_ORDER, i)
+        zs = i
         for kind in (1, 2, 4, 5):
             gat_in(kind, i).wait_recv()
         acc_g[...] = jnp.zeros_like(acc_g)
@@ -258,7 +273,7 @@
             rs_left(i).start()
 
     def stage_s(i):
-        zs = plane(SRC_ORDER, i)
+        zs = i
         rs_far(i).wait()
         role = 1 if i % 2 == 0 else 3
         dxs[role, zs] = (dxs[role, zs].astype(F32) + far_in[zs].astype(F32)).astype(BF16)
@@ -267,27 +282,33 @@
         else:
             rs_right(i).start()
 
-    def back(s):
-        return pltpu.make_async_remote_copy(
-            src_ref=ret.at[s], dst_ref=ret_in.at[me], send_sem=ret_s.at[s], recv_sem=ret_r.at[me],
-            device_id=(s, t), device_id_type=MESH)
-
-    def back_in(o):
-        return pltpu.make_async_remote_copy(
-            src_ref=ret.at[o], dst_ref=ret_in.at[o], send_sem=ret_s.at[o], recv_sem=ret_r.at[o],
-            device_id=(o, t), device_id_type=MESH)
+    def back(i, j):
+        return pltpu.make_async_remote_copy(
+            src_ref=ret.at[i * PL + j], dst_ref=ret_in.at[i * PL + j // 2 * 2 + core],
+            send_sem=ret_s.at[i * PL + j], recv_sem=ret_r.at[i * PL + j // 2 * 2 + core],
+            device_id=(source(i, j), t), device_id_type=MESH)
+
+    def back_in(i, j):
+        return pltpu.make_async_remote_copy(
+            src_ref=ret.at[i * PL + j], dst_ref=ret_in.at[i * PL + j],
+            send_sem=ret_s.at[i * PL + j], recv_sem=ret_r.at[i * PL + j],
+            device_id=(dest(i, j), t), device_id_type=MESH)
 
     def stage_e(i):
-        zs = plane(SRC_ORDER, i)
+        zs = i
         rs_left(i).wait()
         rs_right(i).wait()
         total = dxs[2, zs].astype(F32) + left_in[zs].astype(F32) + right_in[zs].astype(F32)
         rows = dot(rx_ref[...], total.astype(BF16))
         for j in range(PL):
-            ret[zs * PL + j] = rows[j * RB : (j + 1) * RB].astype(BF16)
+            ret[i * PL + j] = rows[j * RB : (j + 1) * RB].astype(BF16)
         if i == 0:
-            ret_in[me] = ret[me]
-        others(zs * PL, lambda s: back(s).start())
+
+            def keep(j):
+                ret_in[j] = ret[j]
+
+            own(keep)
+        others(i, lambda j: back(i, j).start())
 
     def turn(w):
         turned[w] = fac[w].reshape(G * GR, FP)[:, 0:F].T
@@ -297,7 +318,11 @@
             rows = xd[w // 2, q].reshape(G * GR, FP)[:, 0:F]
             grads[w, :, q * F : (q + 1) * F] = dot(turned[w], rows).astype(BF16)
 
+    stage_b(0)
+    stage_b(1)
+    stage_b(2)
     stage_d(0)
+    stage_b(3)
     stage_d(1)
     cut(0)
     stage_f(0)
@@ -340,22 +365,16 @@
         for kind in range(6):
             gat_out(kind, i).wait_send()
 
-    def finish(o, c):
-        @pl.when(o != me)
-        def _():
-            a2a(o).wait_send()
-            back(o).wait_send()
-            back_in(o).wait_recv()
-
-        return c
-
-    lax.fori_loop(0, NDP, finish, 0)
-
-    def hand_on(o, c):
-        back_out[o] = ret_in[o]
-        return c
-
-    lax.fori_loop(0, NDP, hand_on, 0)
+    for i in range(G):
+
+        def finish(j):
+            a2a(i, j).wait_send()
+            back(i, j).wait_send()
+            back_in(i, j).wait_recv()
+
+        others(i, finish)
+        for j in range(PL):
+            back_out[dest(i, j)] = ret_in[i * PL + j]
 
 
 def combine_kernel(
@@ -384,10 +403,11 @@
 
 def tables():
     r = np.arange(PL * SB)
-    jj = r % SB
-    jx = np.where(jj < CAP, jj, -5)
-    jd = np.where((jj >= DOFF) & (jj < DOFF + CAP), jj - DOFF, -5)
-    c40 = np.stack([r // SB, jx, jd], axis=1).astype(np.int32)
+    jj, j = r % SB, r // SB
+    columns = [np.where(jj < CAP, jj, -5), np.where((jj >= DOFF) & (jj < DOFF + CAP), jj - DOFF, -5)]
+    for chips in NEAR:
+        columns += [np.array(chips)[j // 2, 0], np.array(chips)[j // 2, 1], j % 2]
+    c40 = np.stack(columns, axis=1).astype(np.int32)
     cx = np.zeros((GR, PL * SB), np.float32)
     cd = np.zeros((GR, PL * SB), np.float32)
     rx = np.zeros((PL * RB, GR), np.float32)

time: 126 us -> 133 us (1.056)
  Pallas kernels: 125 us -> 132 us
    pallas_call x1, Pallas kernels: 119 us -> 126 us  [shards(): pl.pallas_call(comm_kernel, out_shape=(pltpu.VMEM((3, F, NT * F), BF16),...]
where the time goes in v3:
time: 133 us; the launch traced here: 132 us
  Pallas kernels  132 us (99%)
    pallas_call x1, Pallas kernels, shards(): pl.pallas_call(comm_kernel, out_shape=(pltpu.VMEM((3, F, NT * F), BF16),...  126 us
    pallas_call x1, Pallas kernels, shards(): pl.pallas_call(combine_kernel, out_shape=(jax.ShapeDtypeStruct((F, TOK),...  5.66 us

profile of v3, /device:TPU:1, one launch (start us, length us, event | category | flops | bytes accessed | tf_op | source)
XLA Modules:
  0.0 132.4 jit_solution(7652226834768591215)
XLA Ops:
  0.6 0.0 copy-start
  0.6 0.0 copy-start.1
  0.7 0.0 copy-start.2
  0.7 125.9 %exchange.1 = (bf16[3,720,2880]{2,1,0:T(8,128)(2,1)S(1)}, bf16[32,24,768]{2,1,0:T(8,128)(2,1)S(1)}) custom-call(s32[4,384]{1,0:T(4,128)} %bitcast.23, s32[1,128]{1,0:T(1,128)} %bitcast.25, bf16[4,384]{1,0:T(4,128)(2,1)} %bitcast.32, bf16[720,384]{1,0:T(8,128)(2,1)} %bitcast.30, bf16[720,384]{1,0:T(8,128)(2,1)} %bitcast.31, ...), custom_call_target="tpu_custom_call" | custom-call | tf_op jit(solution)/shard_map/exchange/pallas_call | solution.py:431
  126.5 0.0 copy-done
  126.5 0.0 copy-done.1
  126.6 0.0 copy-done.2
  126.6 5.7 %combine.1 = (bf16[720,384]{1,0:T(8,128)(2,1)}, bf16[720,2880]{1,0:T(8,128)(2,1)}, bf16[720,2880]{1,0:T(8,128)(2,1)}, bf16[720,2880]{1,0:T(8,128)(2,1)}, bf16[4,384]{1,0:T(4,128)(2,1)}) custom-call(s32[4,384]{1,0:T(4,128)S(1)} %bitcast.24, s32[1,128]{1,0:T(1,128)S(1)} %bitcast.26, s32[768,2]{1,0:T(8,128)S(1)} %copy-done, bf16[768,768]{1,0:T(8,128)(2,1)S(1)} %bitcast.22, ...), custom_call_target="tpu_custom_call" | custom-call | tf_op jit(solution)/shard_map/combine/pallas_call | solution.py:460
Async XLA Ops:
  0.6 125.9 %copy-start = (s32[768,2]{1,0:T(8,128)S(1)}, s32[768,2]{1,0:T(8,128)}, u32[]{:S(2)}) copy-start(s32[768,2]{1,0:T(8,128)} %constant.14.clone.c24_ref) | copy-start | bytes 18436
  0.6 125.9 %copy-start.1 = (s32[384,4]{0,1:T(4,128)S(1)}, s32[384,4]{0,1:T(4,128)}, u32[]{:S(2)}) copy-start(s32[384,4]{0,1:T(4,128)} %param.16) | copy-start | bytes 18436
  0.7 125.9 %copy-start.2 = (s32[128]{0:T(128)S(1)}, s32[128]{0:T(128)}, u32[]{:S(2)}) copy-start(s32[128]{0:T(128)} %param.17) | copy-start | bytes 1540

commit v4 on v2

--- a/solution.py
+++ b/solution.py
@@ -20,8 +20,8 @@
 GR = PL * CAP
 WR, WCH = 144, 5
 EXCHANGE_VMEM, COMBINE_VMEM = 48 * 2**20, 16 * 2**20
-SRC_ORDER = (0, 1, 3, 2)
-DST_ORDER = (0, 3, 1, 2)
+SRC_ORDER = (0, 1, 2, 3)
+DST_ORDER = (0, 3, 2, 1)
 LANES = (((1,), (1,)), ((), ()))
 F32, BF16 = jnp.float32, jnp.bfloat16
 
@@ -140,7 +140,7 @@
 
         lax.fori_loop(0, PL, body, 0)
 
-    for i in range(G):
+    def stage_b(i):
         zd = plane(DST_ORDER, i)
         build(zd)
         if i == 0:
@@ -250,8 +250,9 @@
             dxs[r, zs, :, F:FP] = prob[:, 0 : FP - F].astype(BF16)
             return c
 
-        lax.fori_loop(0, NT, backward, 0)
+        backward(0, 0)
         rs_far(i).start()
+        lax.fori_loop(1, NT, backward, 0)
         if i % 2 == 0:
             rs_right(i).start()
         else:
@@ -297,15 +298,19 @@
             rows = xd[w // 2, q].reshape(G * GR, FP)[:, 0:F]
             grads[w, :, q * F : (q + 1) * F] = dot(turned[w], rows).astype(BF16)
 
+    stage_b(0)
+    stage_b(1)
+    stage_b(2)
     stage_d(0)
+    stage_b(3)
     stage_d(1)
     cut(0)
     stage_f(0)
+    cut(1)
+    stage_f(1)
     stage_d(2)
-    stage_f(1)
-    cut(1)
+    cut(2)
     stage_d(3)
-    cut(2)
     stage_c(0)
     stage_f(2)
     stage_c(1)

time: 126 us -> 127 us (level)
  no operation moved by 1% of the time
where the time goes in v4:
time: 127 us; the launch traced here: 126 us
  Pallas kernels  126 us (99%)
    pallas_call x1, Pallas kernels, shards(): pl.pallas_call(comm_kernel, out_shape=(pltpu.VMEM((3, F, NT * F), BF16),...  120 us
    pallas_call x1, Pallas kernels, shards(): pl.pallas_call(combine_kernel, out_shape=(jax.ShapeDtypeStruct((F, TOK),...  5.66 us

profile of v4, /device:TPU:1, one launch (start us, length us, event | category | flops | bytes accessed | tf_op | source)
XLA Modules:
  0.0 126.4 jit_solution(16344563010531242077)
XLA Ops:
  0.6 0.0 copy-start
  0.6 0.0 copy-start.1
  0.7 0.0 copy-start.2
  0.7 119.8 %exchange.1 = (bf16[3,720,2880]{2,1,0:T(8,128)(2,1)S(1)}, bf16[32,24,768]{2,1,0:T(8,128)(2,1)S(1)}) custom-call(s32[4,384]{1,0:T(4,128)} %bitcast.23, s32[1,128]{1,0:T(1,128)} %bitcast.25, bf16[4,384]{1,0:T(4,128)(2,1)} %bitcast.32, bf16[720,384]{1,0:T(8,128)(2,1)} %bitcast.30, bf16[720,384]{1,0:T(8,128)(2,1)} %bitcast.31, s32[320,3]{1,0:T(8,128)} %constant.10.clone.c40_ref, ...), custom_call_target="tpu_custom_call" | custom-call | tf_op jit(solution)/shard_map/exchange/pallas_call | solution.py:416
  120.5 0.0 copy-done
  120.5 0.0 copy-done.1
  120.5 0.0 copy-done.2
  120.6 5.7 %combine.1 = (bf16[720,384]{1,0:T(8,128)(2,1)}, bf16[720,2880]{1,0:T(8,128)(2,1)}, bf16[720,2880]{1,0:T(8,128)(2,1)}, bf16[720,2880]{1,0:T(8,128)(2,1)}, bf16[4,384]{1,0:T(4,128)(2,1)}) custom-call(s32[4,384]{1,0:T(4,128)S(1)} %bitcast.24, s32[1,128]{1,0:T(1,128)S(1)} %bitcast.26, s32[768,2]{1,0:T(8,128)S(1)} %copy-done, bf16[768,768]{1,0:T(8,128)(2,1)S(1)} %bitcast.22, ...), custom_call_target="tpu_custom_call" | custom-call | tf_op jit(solution)/shard_map/combine/pallas_call | solution.py:445
Async XLA Ops:
  0.6 119.9 %copy-start = (s32[768,2]{1,0:T(8,128)S(1)}, s32[768,2]{1,0:T(8,128)}, u32[]{:S(2)}) copy-start(s32[768,2]{1,0:T(8,128)} %constant.14.clone.c24_ref) | copy-start | bytes 18436
  0.6 119.9 %copy-start.1 = (s32[384,4]{0,1:T(4,128)S(1)}, s32[384,4]{0,1:T(4,128)}, u32[]{:S(2)}) copy-start(s32[384,4]{0,1:T(4,128)} %param.16) | copy-start | bytes 18436
  0.7 119.9 %copy-start.2 = (s32[128]{0:T(128)S(1)}, s32[128]{0:T(128)}, u32[]{:S(2)}) copy-start(s32[128]{0:T(128)} %param.17) | copy-start | bytes 1540
